TPU v7x, 32 devices: a whole 2x2x4 slice. The times are simulated.
32 devices in a mesh: dp: 8 (over y, x, core), rep: 4 (over z).
Axes of the slice: x: 2, y: 2, z: 4, core: 2. Of those that a mesh axis runs over, the one named last changes fastest.
Arguments:
- images: bfloat16 [50176, 1024], P(('dp', 'rep')), may hold values from -12 to 12, as said below
- w_reduce: bfloat16 [2, 1024, 256], P(None, 'dp'), may hold values from -0.1875 to 0.1875
- w_spatial: bfloat16 [2, 2304, 256], P(None, 'dp'), may hold values from -0.125 to 0.125
- w_expand: bfloat16 [2, 256, 1024], P(None, 'dp'), may hold values from -0.375 to 0.375
- gammas: float32 [6, 1024], replicated, may hold values from 0.5 to 1.5
- betas: float32 [6, 1024], replicated, may hold values from -1.5 to 1.5
- momenta: float32 [6], replicated, may hold values from 0.2 to 0.9
- run_mean: float32 [8, 1024], P('dp'), may hold values from -3 to 3
- run_var: float32 [8, 1024], P('dp'), may hold values from 0.25 to 4
- slot_table: int32 [8], replicated, may hold values from 0 to 7, each once
Outputs:
- activations: bfloat16 [50176, 1024], P(('dp', 'rep'))
- new_mean: float32 [8, 1024], P('dp')
- new_var: float32 [8, 1024], P('dp')
Inputs may be any that keep to these rules, and one draw needn't show every extreme that they name: `slot_table`: each slot appears once. `images`: each image has its own scale and per-channel offset.
All inputs are finite; a program needn't handle non-finite values.
Results may differ from a plain program's by a relative error of at most 0.0056.
Values may be sent and summed in bfloat16 or wider, within the bound.
A program may use at most 128 MiB of HBM per device.

v0:
```python
import jax
import jax.numpy as jnp
from jax import lax
from jax.sharding import PartitionSpec as P

SIDE = 14
BLOCKS = 2
EPSILON = 0.05
RATIO_MAX = 3.0
SHIFT_MAX = 5.0


def spread(value, axis, source):
    kept = jnp.where(lax.axis_index(axis) == source, value, 0).astype(value.dtype)
    return lax.psum(kept, axis)


def conv_patches(hidden):
    count = hidden.shape[0] // (SIDE * SIDE)
    channels = hidden.shape[1]
    shaped = hidden.reshape(count, SIDE, SIDE, channels)
    padded = jnp.pad(shaped, ((0, 0), (1, 1), (1, 1), (0, 0)))
    pieces = [
        padded[:, row_off : row_off + SIDE, col_off : col_off + SIDE, :]
        for row_off in range(3)
        for col_off in range(3)
    ]
    return jnp.concatenate(pieces, axis=-1).reshape(count * SIDE * SIDE, 9 * channels)


def renorm_factors(total, squares, count, run_m, run_v, gain, offset):
    batch_mean = total / count
    batch_var = jnp.maximum(squares / count - batch_mean * batch_mean, 0.0)
    batch_sigma = jnp.sqrt(batch_var + EPSILON)
    run_sigma = jnp.sqrt(run_v + EPSILON)
    ratio = jnp.clip(batch_sigma / run_sigma, 1.0 / RATIO_MAX, RATIO_MAX)
    shift = jnp.clip((batch_mean - run_m) / run_sigma, -SHIFT_MAX, SHIFT_MAX)
    scale = gain * ratio / batch_sigma
    bias = offset + gain * (shift - ratio * batch_mean / batch_sigma)
    return (scale, bias, batch_mean, batch_var)


def whole_weight(shard):
    return lax.all_gather(shard, "dp", axis=0, tiled=True)


def channel_moments(pre):
    total = jnp.sum(pre, axis=0)
    squares = jnp.sum(pre * pre, axis=0)
    total, squares = lax.psum((total, squares), "rep")
    total, squares = lax.psum((total, squares), "dp")
    return (total, squares)


def body(
    images, w_reduce, w_spatial, w_expand, gammas, betas, momenta, run_mean, run_var, slot_table
):
    own_index = lax.axis_index("dp")
    count = 1.0 * images.shape[0] * lax.axis_size("dp") * lax.axis_size("rep")
    base_mean = run_mean[0]
    base_var = run_var[0]

    def running(layer_index):
        return (
            spread(base_mean, "dp", slot_table[layer_index]),
            spread(base_var, "dp", slot_table[layer_index]),
        )

    updates = []

    def layer_norm(pre, layer_index):
        channels = pre.shape[1]
        total, squares = channel_moments(pre)
        state_mean, state_var = running(layer_index)
        run_m = state_mean[:channels]
        run_v = state_var[:channels]
        scale, bias, batch_mean, batch_var = renorm_factors(
            total,
            squares,
            count,
            run_m,
            run_v,
            gammas[layer_index, :channels],
            betas[layer_index, :channels],
        )
        rate = momenta[layer_index]
        updates.append(
            (
                layer_index,
                channels,
                run_m + rate * (batch_mean - run_m),
                run_v + rate * (batch_var - run_v),
            )
        )
        return pre * scale + bias

    current = images
    for block_index in range(BLOCKS):
        first = 3 * block_index
        pre = jnp.dot(
            current, whole_weight(w_reduce[block_index]), preferred_element_type=jnp.float32
        )
        hidden = jax.nn.relu(layer_norm(pre, first)).astype(jnp.bfloat16)
        patches = conv_patches(hidden)
        pre = jnp.dot(
            patches, whole_weight(w_spatial[block_index]), preferred_element_type=jnp.float32
        )
        spatial = jax.nn.relu(layer_norm(pre, first + 1)).astype(jnp.bfloat16)
        pre = jnp.dot(
            spatial, whole_weight(w_expand[block_index]), preferred_element_type=jnp.float32
        )
        normed = layer_norm(pre, first + 2)
        current = jax.nn.relu(normed + current.astype(jnp.float32)).astype(jnp.bfloat16)
    out_mean = base_mean
    out_var = base_var
    for layer_index, channels, fresh_mean, fresh_var in updates:
        owned_here = slot_table[layer_index] == own_index
        full_mean = jnp.concatenate([fresh_mean, base_mean[channels:]])
        full_var = jnp.concatenate([fresh_var, base_var[channels:]])
        out_mean = jnp.where(owned_here, full_mean, out_mean)
        out_var = jnp.where(owned_here, full_var, out_var)
    return (current, out_mean[None], out_var[None])


def solution(mesh):
    in_specs = (
        P(("dp", "rep"), None),
        P(None, "dp", None),
        P(None, "dp", None),
        P(None, "dp", None),
        P(),
        P(),
        P(),
        P("dp", None),
        P("dp", None),
        P(),
    )
    out_specs = (P(("dp", "rep"), None), P("dp", None), P("dp", None))
    return jax.shard_map(body, mesh=mesh, in_specs=in_specs, out_specs=out_specs, check_vma=False)
```

profile of v0, /device:TPU:0, one launch (start us, length us, event | category | flops | bytes accessed | tf_op | source)
XLA Modules:
  0.0 399.4 jit_solution(15535920908648525998)
XLA Ops:
  7.2 1.7 fusion.24
  9.7 1.4 fusion.29
  12.0 1.4 fusion.30
  14.3 1.6 fusion.32
  24.5 13.1 %all-gather = bf16[1,1024,256]{2,1,0:T(8,128)(2,1)S(1)} all-gather(bf16[1,128,256]{2,1,0:T(8,128)(2,1)S(1)} %get-tuple-element.72), channel_id=2, replica_groups=mesh['dp'=8,'rep'=4] {'dp'}, dimensions={1}, use_global_device_ids=true | all-gather | bytes 589824 | tf_op jit(solution)/shard_map/all_gather | solution.py:44
  37.6 1.5 fusion.31
  40.5 2.9 multiply_reduce_fusion.5
  43.5 11.8 %all-reduce.13 = (f32[256]{0:T(256)S(1)}, f32[256]{0:T(256)S(1)}) all-reduce(f32[256]{0:T(256)S(1)} %get-tuple-element.14, f32[256]{0:T(256)S(1)} %get-tuple-element.13), channel_id=1, replica_groups=mesh['dp'=8,'rep'=4] {'rep'}, use_global_device_ids=true, to_apply=%region_4.0 | all-reduce | flops 512 | bytes 4096 | tf_op jit(solution)/shard_map/psum | solution.py:50
  55.9 22.6 %all-reduce.7 = (f32[1024]{0:T(1024)S(1)}, f32[256]{0:T(256)S(1)}, f32[1024]{0:T(1024)S(1)}, f32[256]{0:T(256)S(1)}) all-reduce(f32[1024]{0:T(1024)S(1)} %get-tuple-element.110, f32[256]{0:T(256)S(1)} %get-tuple-element.49, f32[1024]{0:T(1024)S(1)} %get-tuple-element.135, ...), channel_id=1, replica_groups=mesh['dp'=8,'rep'=4] {'dp'}, use_global_device_ids=true, to_apply=%region_7.8 | all-reduce | flops 2560 | bytes 20480 | tf_op jit(solution)/shard_map/psum | solution.py:15
  78.5 1.2 multiply_divide_fusion.5
  80.3 1.1 reshape.48
  81.4 6.8 %pad_slice_fusion.8 = (bf16[8,14,14,256]{3,2,1,0:T(8,128)(2,1)S(1)}, bf16[8,14,14,256]{3,2,1,0:T(8,128)(2,1)}, bf16[8,14,14,256]{3,2,1,0:T(8,128)(2,1)}, bf16[8,...) fusion(bf16[8,14,14,256]{3,2,1,0:T(8,128)(2,1)} %reshape.48), kind=kLoop, calls=%fused_computation.32 | loop fusion | bytes 7225344 | tf_op jit(solution)/shard_map/slice | solution.py:24
  88.2 2.1 concatenate.64
  90.3 2.2 constant_dynamic-update-slice_fusion.8
  92.5 2.1 concatenate.65
  94.6 2.1 concatenate.66
  96.7 2.1 concatenate.67
  98.9 2.1 constant_dynamic-update-slice_fusion.7
  101.0 2.1 constant_dynamic-update-slice_fusion.6
  103.2 2.1 constant_dynamic-update-slice_fusion.5
  105.3 1.8 constant_dynamic-update-slice_fusion.4
  107.1 2.1 concatenate.68
  109.2 2.1 concatenate.69
  112.7 9.4 %all-gather.2 = bf16[1,256,1024]{2,1,0:T(8,128)(2,1)S(1)} all-gather(bf16[1,32,1024]{2,1,0:T(8,128)(2,1)S(1)} %get-tuple-element.70), channel_id=4, replica_groups=mesh['dp'=8,'rep'=4] {'dp'}, dimensions={1}, use_global_device_ids=true | all-gather | bytes 589824 | tf_op jit(solution)/shard_map/all_gather | solution.py:44
  122.1 10.3 %all-gather.3 = bf16[1,1024,256]{2,1,0:T(8,128)(2,1)} all-gather(bf16[1,128,256]{2,1,0:T(8,128)(2,1)S(1)} %get-tuple-element.71), channel_id=5, replica_groups=mesh['dp'=8,'rep'=4] {'dp'}, dimensions={1}, use_global_device_ids=true | all-gather | bytes 589824 | tf_op jit(solution)/shard_map/all_gather | solution.py:44
  132.4 10.4 %all-gather.5 = bf16[1,256,1024]{2,1,0:T(8,128)(2,1)} all-gather(bf16[1,32,1024]{2,1,0:T(8,128)(2,1)S(1)} %get-tuple-element.69), channel_id=7, replica_groups=mesh['dp'=8,'rep'=4] {'dp'}, dimensions={1}, use_global_device_ids=true | all-gather | bytes 589824 | tf_op jit(solution)/shard_map/all_gather | solution.py:44
  142.7 2.1 constant_dynamic-update-slice_fusion.3
  144.8 2.2 constant_dynamic-update-slice_fusion.2
  149.1 5.4 %multiply_reduce_fusion.4 = (f32[256]{0:T(256)S(1)}, f32[256]{0:T(256)S(1)}, f32[1568,256]{1,0:T(8,128)S(1)}) fusion(bf16[1568,2304]{1,0:T(8,128)(2,1)} %constant_dynamic-update-slice_fusion, bf16[1,2304,256]{2,1,0:T(8,128)(2,1)} %all-gather.9.cloned.1.call-done), kind=kOutput, calls=%fused_computation.9 | convolution fusion | flops 1850891776 | bytes 10012672 | tf_op jit(solution)/shard_map/dot_general | solution.py:105
  154.5 8.4 %all-reduce.12 = (f32[256]{0:T(256)S(1)}, f32[256]{0:T(256)S(1)}) all-reduce(f32[256]{0:T(256)S(1)} %get-tuple-element.12, f32[256]{0:T(256)S(1)} %get-tuple-element.11), channel_id=1, replica_groups=mesh['dp'=8,'rep'=4] {'rep'}, use_global_device_ids=true, to_apply=%region_12.13 | all-reduce | flops 512 | bytes 4096 | tf_op jit(solution)/shard_map/psum | solution.py:50
  162.9 22.5 %all-reduce.6 = (f32[1024]{0:T(1024)S(1)}, f32[256]{0:T(256)S(1)}, f32[1024]{0:T(1024)S(1)}, f32[256]{0:T(256)S(1)}) all-reduce(f32[1024]{0:T(1024)S(1)} %copy-done.6, f32[256]{0:T(256)S(1)} %get-tuple-element.47, f32[1024]{0:T(1024)S(1)} %copy-done.7, f32[256]{0:T(256)S(1)} %get-tuple-element.48), channel_id=1, replica_groups=mesh['dp'=8,'rep'=4] {'dp'}, use_global_device_ids=true, to_apply=%region_15.16 | all-reduce | flops 2560 | bytes 20480 | tf_op jit(solution)/shard_map/psum | solution.py:15
  186.1 3.8 multiply_reduce_fusion.1
  189.9 10.5 %all-reduce.11 = (f32[1024]{0:T(1024)S(1)}, f32[1024]{0:T(1024)S(1)}) all-reduce(f32[1024]{0:T(1024)S(1)} %get-tuple-element.6, f32[1024]{0:T(1024)S(1)} %get-tuple-element.5), channel_id=1, replica_groups=mesh['dp'=8,'rep'=4] {'rep'}, use_global_device_ids=true, to_apply=%region_20.21 | all-reduce | flops 2048 | bytes 16384 | tf_op jit(solution)/shard_map/psum | solution.py:50
  200.4 22.3 %all-reduce.5 = (f32[1024]{0:T(1024)S(1)}, f32[1024]{0:T(1024)S(1)}, f32[1024]{0:T(1024)S(1)}, f32[1024]{0:T(1024)S(1)}) all-reduce(f32[1024]{0:T(1024)S(1)} %copy-done.11, f32[1024]{0:T(1024)S(1)} %get-tuple-element.45, f32[1024]{0:T(1024)S(1)} %copy-done.10, f32[1024]{0:T(1024)S(1)} %get-tuple-element.46), channel_id=1, replica_groups=mesh['dp'=8,'rep'=4] {'dp'}, use_global_device_ids=true, to_apply=%region_22.23 | all-reduce | flops 4096 | bytes 32768 | tf_op jit(solution)/shard_map/psum | solution.py:15
  222.8 5.2 %maximum_convert_fusion.1 = bf16[1568,1024]{1,0:T(8,128)(2,1)S(1)} fusion(bf16[1568,1024]{1,0:T(8,128)(2,1)} %param.10, f32[1568,1024]{1,0:T(8,128)} %get-tuple-element.131, f32[1024]{0:T(1024)S(1)} %get-tuple-element.88, f32[1024]{0:T(1024)S(1)} %get-tuple-element.87), kind=kLoop, calls=%fused_computation.2 | loop fusion | flops 9633792 | bytes 12853248 | tf_op jit(solution)/shard_map/convert_element_type | solution.py:113
  228.0 2.2 multiply_reduce_fusion.3
  230.1 8.3 %all-reduce.10 = (f32[256]{0:T(256)S(1)}, f32[256]{0:T(256)S(1)}) all-reduce(f32[256]{0:T(256)S(1)} %get-tuple-element.10, f32[256]{0:T(256)S(1)} %get-tuple-element.9), channel_id=1, replica_groups=mesh['dp'=8,'rep'=4] {'rep'}, use_global_device_ids=true, to_apply=%region_28.29 | all-reduce | flops 512 | bytes 4096 | tf_op jit(solution)/shard_map/psum | solution.py:50
  238.5 22.3 %all-reduce.4 = (f32[1024]{0:T(1024)S(1)}, f32[256]{0:T(256)S(1)}, f32[1024]{0:T(1024)S(1)}, f32[256]{0:T(256)S(1)}) all-reduce(f32[1024]{0:T(1024)S(1)} %get-tuple-element.107, f32[256]{0:T(256)S(1)} %get-tuple-element.43, f32[1024]{0:T(1024)S(1)} %get-tuple-element.138, ...), channel_id=1, replica_groups=mesh['dp'=8,'rep'=4] {'dp'}, use_global_device_ids=true, to_apply=%region_31.32 | all-reduce | flops 2560 | bytes 20480 | tf_op jit(solution)/shard_map/psum | solution.py:15
  261.4 2.5 maximum_convert_fusion.3
  264.0 2.1 reshape.49
  266.1 7.0 %pad_slice_fusion = (bf16[8,14,14,256]{3,2,1,0:T(8,128)(2,1)}, bf16[8,14,14,256]{3,2,1,0:T(8,128)(2,1)}, bf16[8,14,14,256]{3,2,1,0:T(8,128)(2,1)}, bf16[8,14,14,...) fusion(bf16[8,14,14,256]{3,2,1,0:T(8,128)(2,1)} %reshape.49), kind=kLoop, calls=%fused_computation.24 | loop fusion | bytes 7225344 | tf_op jit(solution)/shard_map/slice | solution.py:24
  273.1 2.1 concatenate.73
  275.2 2.2 constant_dynamic-update-slice_fusion.17
  277.4 2.1 concatenate.74
  279.6 2.1 constant_dynamic-update-slice_fusion.16
  281.7 2.1 concatenate.75
  283.8 2.2 concatenate.76
  286.0 2.1 concatenate.77
  288.1 2.1 concatenate.78
  290.2 2.1 concatenate.79
  292.4 2.1 concatenate.80
  294.5 2.3 constant_dynamic-update-slice_fusion.15
  296.8 2.1 constant_dynamic-update-slice_fusion.14
  298.9 2.6 constant_dynamic-update-slice_fusion.13
  301.5 2.1 constant_dynamic-update-slice_fusion.12
  306.7 6.5 %multiply_reduce_fusion.2 = (f32[256]{0:T(256)S(1)}, f32[256]{0:T(256)S(1)}, f32[1568,256]{1,0:T(8,128)}) fusion(bf16[1568,2304]{1,0:T(8,128)(2,1)} %constant_dynamic-update-slice_fusion.9, bf16[1,2304,256]{2,1,0:T(8,128)(2,1)} %all-gather.11.cloned.1.call-done), kind=kOutput, calls=%fused_computation.5 | convolution fusion | flops 1850891776 | bytes 10012672 | tf_op jit(solution)/shard_map/dot_general | solution.py:105
  313.3 10.3 %all-reduce.9 = (f32[256]{0:T(256)S(1)}, f32[256]{0:T(256)S(1)}) all-reduce(f32[256]{0:T(256)S(1)} %get-tuple-element.8, f32[256]{0:T(256)S(1)} %get-tuple-element.7), channel_id=1, replica_groups=mesh['dp'=8,'rep'=4] {'rep'}, use_global_device_ids=true, to_apply=%region_36.37 | all-reduce | flops 512 | bytes 4096 | tf_op jit(solution)/shard_map/psum | solution.py:50
  323.6 22.5 %all-reduce.3 = (f32[1024]{0:T(1024)S(1)}, f32[256]{0:T(256)S(1)}, f32[1024]{0:T(1024)S(1)}, f32[256]{0:T(256)S(1)}) all-reduce(f32[1024]{0:T(1024)S(1)} %get-tuple-element.106, f32[256]{0:T(256)S(1)} %get-tuple-element.41, f32[1024]{0:T(1024)S(1)} %get-tuple-element.139, ...), channel_id=1, replica_groups=mesh['dp'=8,'rep'=4] {'dp'}, use_global_device_ids=true, to_apply=%region_39.40 | all-reduce | flops 2560 | bytes 20480 | tf_op jit(solution)/shard_map/psum | solution.py:15
  346.8 5.3 %multiply_reduce_fusion = (f32[1024]{0:T(1024)S(1)}, f32[1024]{0:T(1024)S(1)}, f32[1568,1024]{1,0:T(8,128)}) fusion(bf16[1,256,1024]{2,1,0:T(8,128)(2,1)} %all-gather.5, f32[1568,256]{1,0:T(8,128)} %get-tuple-element.133, f32[256]{0:T(256)S(1)} %get-tuple-element.90, f32[256]{0:T(256)S(1)} %get-tuple-element.89), kind=kOutput, calls=%fused_computation.1 | convolution fusion | flops 828504064 | bytes 8562688 | tf_op jit(solution)/shard_map/dot_general | solution.py:109
  352.1 8.5 %all-reduce.8 = (f32[1024]{0:T(1024)S(1)}, f32[1024]{0:T(1024)S(1)}) all-reduce(f32[1024]{0:T(1024)S(1)} %get-tuple-element.4, f32[1024]{0:T(1024)S(1)} %get-tuple-element.3), channel_id=1, replica_groups=mesh['dp'=8,'rep'=4] {'rep'}, use_global_device_ids=true, to_apply=%region_44.45 | all-reduce | flops 2048 | bytes 16384 | tf_op jit(solution)/shard_map/psum | solution.py:50
  360.6 22.3 %all-reduce.2 = (f32[1024]{0:T(1024)S(1)}, f32[1024]{0:T(1024)S(1)}, f32[1024]{0:T(1024)S(1)}, f32[1024]{0:T(1024)S(1)}) all-reduce(f32[1024]{0:T(1024)S(1)} %copy-done.9, f32[1024]{0:T(1024)S(1)} %get-tuple-element.39, f32[1024]{0:T(1024)S(1)} %copy-done.8, f32[1024]{0:T(1024)S(1)} %get-tuple-element.40), channel_id=1, replica_groups=mesh['dp'=8,'rep'=4] {'dp'}, use_global_device_ids=true, to_apply=%region_46.47 | all-reduce | flops 4096 | bytes 32768 | tf_op jit(solution)/shard_map/psum | solution.py:15
  383.0 5.8 %maximum_convert_fusion = bf16[1568,1024]{1,0:T(8,128)(2,1)} fusion(bf16[1568,1024]{1,0:T(8,128)(2,1)S(1)} %maximum_convert_fusion.1, f32[1568,1024]{1,0:T(8,128)} %get-tuple-element.134, f32[1024]{0:T(1024)S(1)} %get-tuple-element.86, f32[1024]{0:T(1024)S(1)} %get-tuple-element.85), kind=kLoop, calls=%fused_computation | loop fusion | flops 9633792 | bytes 12853248 | tf_op jit(solution)/shard_map/convert_element_type | solution.py:113
  388.8 1.9 fusion.20
  390.7 1.9 fusion.18
  (70 shorter events, 14.6 us)
Async XLA Ops:
  7.2 48.1 %copy-start.5 = (f32[1,1024]{1,0:T(1,128)S(1)}, f32[1,1024]{1,0:T(1,128)}, u32[]{:S(2)}) copy-start(f32[1,1024]{1,0:T(1,128)} %param.18) | copy-start | bytes 12292
  7.2 48.1 %copy-start.4 = (f32[1,1024]{1,0:T(1,128)S(1)}, f32[1,1024]{1,0:T(1,128)}, u32[]{:S(2)}) copy-start(f32[1,1024]{1,0:T(1,128)} %param.17) | copy-start | bytes 12292
  7.2 141.9 %all-gather.9.cloned.1.call-start = ((), (), s32[]{:S(2)}) async-start(), calls=%async_computation | async-start | bytes 1327104 | tf_op jit(solution)/shard_map/all_gather | solution.py:44
  9.0 297.7 %all-gather.11.cloned.1.call-start = ((), (), s32[]{:S(2)}) async-start(), calls=%async_computation.1 | async-start | bytes 1327104 | tf_op jit(solution)/shard_map/all_gather | solution.py:44
  79.7 0.6 copy-start.12
  79.7 0.6 copy-start.13
  149.1 13.8 %copy-start.6 = (f32[1024]{0:T(1024)S(1)}, f32[1024]{0:T(1024)}, u32[]{:S(2)}) copy-start(f32[1024]{0:T(1024)} %get-tuple-element.109) | copy-start | bytes 12292
  149.1 13.8 %copy-start.7 = (f32[1024]{0:T(1024)S(1)}, f32[1024]{0:T(1024)}, u32[]{:S(2)}) copy-start(f32[1024]{0:T(1024)} %get-tuple-element.136) | copy-start | bytes 12292
  149.1 36.3 %copy-start.20 = (f32[1,256]{1,0:T(1,128)S(1)}, f32[1,256]{1,0:T(1,128)}, u32[]{:S(2)}) copy-start(f32[1,256]{1,0:T(1,128)} %get-tuple-element.79) | copy-start | bytes 3076
  149.1 36.3 %copy-start.21 = (f32[1,256]{1,0:T(1,128)S(1)}, f32[1,256]{1,0:T(1,128)}, u32[]{:S(2)}) copy-start(f32[1,256]{1,0:T(1,128)} %get-tuple-element.83) | copy-start | bytes 3076
  186.1 14.3 %copy-start.10 = (f32[1024]{0:T(1024)S(1)}, f32[1024]{0:T(1024)}, u32[]{:S(2)}) copy-start(f32[1024]{0:T(1024)} %get-tuple-element.108) | copy-start | bytes 12292
  186.1 14.3 %copy-start.11 = (f32[1024]{0:T(1024)S(1)}, f32[1024]{0:T(1024)}, u32[]{:S(2)}) copy-start(f32[1024]{0:T(1024)} %get-tuple-element.137) | copy-start | bytes 12292
  222.8 5.2 %copy-start.3 = (bf16[1,1024,256]{2,1,0:T(8,128)(2,1)S(1)}, bf16[1,1024,256]{2,1,0:T(8,128)(2,1)}, u32[]{:S(2)}) copy-start(bf16[1,1024,256]{2,1,0:T(8,128)(2,1)} %all-gather.3) | copy-start | bytes 1572868
  228.0 32.8 %copy-start.18 = (f32[1,256]{1,0:T(1,128)S(1)}, f32[1,256]{1,0:T(1,128)}, u32[]{:S(2)}) copy-start(f32[1,256]{1,0:T(1,128)} %get-tuple-element.78) | copy-start | bytes 3076
  228.0 32.8 %copy-start.19 = (f32[1,256]{1,0:T(1,128)S(1)}, f32[1,256]{1,0:T(1,128)}, u32[]{:S(2)}) copy-start(f32[1,256]{1,0:T(1,128)} %get-tuple-element.82) | copy-start | bytes 3076
  294.5 9.1 %copy-start.2 = (bf16[1568,256]{1,0:T(8,128)(2,1)S(1)}, bf16[1568,256]{1,0:T(8,128)(2,1)}, u32[]{:S(2)}) copy-start(bf16[1568,256]{1,0:T(8,128)(2,1)} %concatenate.78) | copy-start | bytes 2408452
  294.5 10.2 %copy-start = (bf16[1568,256]{1,0:T(8,128)(2,1)S(1)}, bf16[1568,256]{1,0:T(8,128)(2,1)}, u32[]{:S(2)}) copy-start(bf16[1568,256]{1,0:T(8,128)(2,1)} %concatenate.79) | copy-start | bytes 2408452
  294.5 11.2 %copy-start.1 = (bf16[1568,256]{1,0:T(8,128)(2,1)S(1)}, bf16[1568,256]{1,0:T(8,128)(2,1)}, u32[]{:S(2)}) copy-start(bf16[1568,256]{1,0:T(8,128)(2,1)} %concatenate.80) | copy-start | bytes 2408452
  306.7 39.4 %copy-start.16 = (f32[1,256]{1,0:T(1,128)S(1)}, f32[1,256]{1,0:T(1,128)}, u32[]{:S(2)}) copy-start(f32[1,256]{1,0:T(1,128)} %get-tuple-element.77) | copy-start | bytes 3076
  306.7 39.4 %copy-start.17 = (f32[1,256]{1,0:T(1,128)S(1)}, f32[1,256]{1,0:T(1,128)}, u32[]{:S(2)}) copy-start(f32[1,256]{1,0:T(1,128)} %get-tuple-element.81) | copy-start | bytes 3076
  346.7 13.8 %copy-start.8 = (f32[1024]{0:T(1024)S(1)}, f32[1024]{0:T(1024)}, u32[]{:S(2)}) copy-start(f32[1024]{0:T(1024)} %get-tuple-element.105) | copy-start | bytes 12292
  346.8 13.8 %copy-start.9 = (f32[1024]{0:T(1024)S(1)}, f32[1024]{0:T(1024)}, u32[]{:S(2)}) copy-start(f32[1024]{0:T(1024)} %get-tuple-element.140) | copy-start | bytes 12292
  383.0 5.8 %copy-start.15 = (f32[256]{0:T(256)S(1)}, f32[256]{0:T(256)}, u32[]{:S(2)}) copy-start(f32[256]{0:T(256)} %get-tuple-element.97) | copy-start | bytes 3076
  383.0 7.7 %copy-start.14 = (f32[256]{0:T(256)S(1)}, f32[256]{0:T(256)}, u32[]{:S(2)}) copy-start(f32[256]{0:T(256)} %get-tuple-element.104) | copy-start | bytes 3076
Sparse Core Ops, SparseCore 0:
  9.9 28.2 all-gather.8
  40.0 24.0 all-gather.10
where the time goes:
time: 401 us; the launch traced here: 399 us
  blocking collectives  236 us (59%)
  local copies, waits for them, and re-layouts  89.3 us (22%)
  matrix products  26.1 us (7%)
  other arithmetic  25.6 us (6%)
  between operations  22 us (5%)
    psum x6, blocking collectives, spread(): return lax.psum(kept, axis)  135 us
    psum x6, blocking collectives, channel_moments(): total, squares = lax.psum((total, squares), 'rep')  57.8 us
    all_gather x4, blocking collectives, whole_weight(): return lax.all_gather(shard, 'dp', axis=0, tiled=True)  43.1 us
    concatenate x18, local copies, waits for them, and re-layouts, conv_patches(): jnp.concatenate(pieces, axis=-1).reshape(count * SIDE * SIDE, 9 * channels)  32.2 us
    unnamed x58, local copies, waits for them, and re-layouts  27.4 us
    slice x2, local copies, waits for them, and re-layouts, conv_patches(): padded[:, row_off:row_off + SIDE, col_off:col_off + SIDE, :]  13.8 us
    dot_general x2, matrix products, body(): jnp.dot(patches, whole_weight(w_spatial[block_index]), preferred_element_...  11.9 us
    convert_element_type x2, other arithmetic, body(): jax.nn.relu(normed + current.astype(jnp.float32)).astype(jnp.bfloat16)  11 us
  transfers between devices with their start and end apart: 2, of which 0 were waited for; matrix products, arithmetic and copies ran while one was open for 29% of the time, Pallas kernels for 0%

commit v1 on v0

--- a/solution.py
+++ b/solution.py
@@ -12,7 +12,7 @@
 
 def spread(value, axis, source):
     kept = jnp.where(lax.axis_index(axis) == source, value, 0).astype(value.dtype)
-    return lax.psum(kept, axis)
+    return jnp.sum(lax.all_gather(kept, axis), axis=0)
 
 
 def conv_patches(hidden):

time: 401 us -> 442 us (1.10)
  blocking collectives: 236 us -> 275 us
    all_gather x0 -> x12, blocking collectives: none -> 106 us  [spread(): return jnp.sum(lax.all_gather(kept, axis), axis=0)]
    psum x6, blocking collectives: 135 us -> 71.6 us  [channel_moments(): total, squares = lax.psum((total, squares), 'dp')]
    unnamed x58 -> x56, local copies, waits for them, and re-layouts: 27.4 us -> 26.3 us
  transfers between devices with their start and end apart: 2 -> 2, of which waited for: 0 -> 0; matrix products, arithmetic and copies ran while one was open for 29% -> 27% of each run, Pallas kernels for 0% -> 0%
where the time goes in v1:
time: 442 us; the launch traced here: 440 us
  blocking collectives  275 us (62%)
  local copies, waits for them, and re-layouts  89.3 us (20%)
  other arithmetic  26.9 us (6%)
  matrix products  26.1 us (6%)
  between operations  22.1 us (5%)
    all_gather x12, blocking collectives, spread(): return jnp.sum(lax.all_gather(kept, axis), axis=0)  106 us
    psum x6, blocking collectives, channel_moments(): total, squares = lax.psum((total, squares), 'dp')  71.6 us
    psum x6, blocking collectives, channel_moments(): total, squares = lax.psum((total, squares), 'rep')  58 us
    all_gather x4, blocking collectives, whole_weight(): return lax.all_gather(shard, 'dp', axis=0, tiled=True)  39.3 us
    concatenate x18, local copies, waits for them, and re-layouts, conv_patches(): jnp.concatenate(pieces, axis=-1).reshape(count * SIDE * SIDE, 9 * channels)  32.2 us
    unnamed x56, local copies, waits for them, and re-layouts  26.3 us
    slice x2, local copies, waits for them, and re-layouts, conv_patches(): padded[:, row_off:row_off + SIDE, col_off:col_off + SIDE, :]  13.8 us
    dot_general x2, matrix products, body(): jnp.dot(patches, whole_weight(w_spatial[block_index]), preferred_element_...  11.9 us
  transfers between devices with their start and end apart: 2, of which 0 were waited for; matrix products, arithmetic and copies ran while one was open for 27% of the time, Pallas kernels for 0%

profile of v1, /device:TPU:0, one launch (start us, length us, event | category | flops | bytes accessed | tf_op | source)
XLA Modules:
  0.0 440.1 jit_solution(12120983131690945256)
XLA Ops:
  27.6 10.8 %all-gather.6 = f32[8,1,1024]{2,1,0:T(1,128)S(1)} all-gather(f32[1,1,1024]{2,1,0:T(1,128)S(1)} %get-tuple-element.104), channel_id=1, replica_groups=mesh['dp'=8,'rep'=4] {'dp'}, dimensions={0}, use_global_device_ids=true | all-gather | bytes 36864 | tf_op jit(solution)/shard_map/all_gather | solution.py:15
  38.4 9.0 %all-gather.7 = f32[8,1,1024]{2,1,0:T(1,128)S(1)} all-gather(f32[1,1,1024]{2,1,0:T(1,128)S(1)} %get-tuple-element.98), channel_id=1, replica_groups=mesh['dp'=8,'rep'=4] {'dp'}, dimensions={0}, use_global_device_ids=true | all-gather | bytes 36864 | tf_op jit(solution)/shard_map/all_gather | solution.py:15
  48.4 9.0 %all-gather = bf16[1,1024,256]{2,1,0:T(8,128)(2,1)S(1)} all-gather(bf16[1,128,256]{2,1,0:T(8,128)(2,1)S(1)} %get-tuple-element.60), channel_id=2, replica_groups=mesh['dp'=8,'rep'=4] {'dp'}, dimensions={1}, use_global_device_ids=true | all-gather | bytes 589824 | tf_op jit(solution)/shard_map/all_gather | solution.py:44
  58.9 3.0 multiply_reduce_fusion.5
  61.8 12.0 %all-reduce.13 = (f32[256]{0:T(256)S(1)}, f32[256]{0:T(256)S(1)}) all-reduce(f32[256]{0:T(256)S(1)} %get-tuple-element.14, f32[256]{0:T(256)S(1)} %get-tuple-element.13), channel_id=1, replica_groups=mesh['dp'=8,'rep'=4] {'rep'}, use_global_device_ids=true, to_apply=%region_4.0 | all-reduce | flops 512 | bytes 4096 | tf_op jit(solution)/shard_map/psum | solution.py:50
  73.8 11.8 %all-reduce.7 = (f32[256]{0:T(256)S(1)}, f32[256]{0:T(256)S(1)}) all-reduce(f32[256]{0:T(256)S(1)} %get-tuple-element.37, f32[256]{0:T(256)S(1)} %get-tuple-element.38), channel_id=1, replica_groups=mesh['dp'=8,'rep'=4] {'dp'}, use_global_device_ids=true, to_apply=%region_5.0 | all-reduce | flops 512 | bytes 4096 | tf_op jit(solution)/shard_map/psum | solution.py:51
  88.5 6.8 %pad_slice_fusion.8 = (bf16[8,14,14,256]{3,2,1,0:T(8,128)(2,1)S(1)}, bf16[8,14,14,256]{3,2,1,0:T(8,128)(2,1)}, bf16[8,14,14,256]{3,2,1,0:T(8,128)(2,1)}, bf16[8,...) fusion(bf16[8,14,14,256]{3,2,1,0:T(8,128)(2,1)} %reshape.48), kind=kLoop, calls=%fused_computation.32 | loop fusion | bytes 7225344 | tf_op jit(solution)/shard_map/slice | solution.py:24
  95.3 2.1 concatenate.64
  97.4 2.2 constant_dynamic-update-slice_fusion.8
  99.6 2.1 concatenate.65
  101.7 2.1 concatenate.66
  103.9 2.1 concatenate.67
  106.0 2.1 constant_dynamic-update-slice_fusion.7
  108.1 2.1 constant_dynamic-update-slice_fusion.6
  110.3 2.1 constant_dynamic-update-slice_fusion.5
  116.3 2.1 concatenate.69
  118.9 8.9 %all-gather.8 = f32[8,1,1024]{2,1,0:T(1,128)S(1)} all-gather(f32[1,1,1024]{2,1,0:T(1,128)S(1)} %get-tuple-element.103), channel_id=1, replica_groups=mesh['dp'=8,'rep'=4] {'dp'}, dimensions={0}, use_global_device_ids=true | all-gather | bytes 36864 | tf_op jit(solution)/shard_map/all_gather | solution.py:15
  127.9 8.3 %all-gather.9 = f32[8,1,1024]{2,1,0:T(1,128)S(1)} all-gather(f32[1,1,1024]{2,1,0:T(1,128)S(1)} %get-tuple-element.97), channel_id=1, replica_groups=mesh['dp'=8,'rep'=4] {'dp'}, dimensions={0}, use_global_device_ids=true | all-gather | bytes 36864 | tf_op jit(solution)/shard_map/all_gather | solution.py:15
  137.1 9.7 %all-gather.2 = bf16[1,256,1024]{2,1,0:T(8,128)(2,1)S(1)} all-gather(bf16[1,32,1024]{2,1,0:T(8,128)(2,1)S(1)} %get-tuple-element.58), channel_id=4, replica_groups=mesh['dp'=8,'rep'=4] {'dp'}, dimensions={1}, use_global_device_ids=true | all-gather | bytes 589824 | tf_op jit(solution)/shard_map/all_gather | solution.py:44
  146.8 8.3 %all-gather.10 = f32[8,1,1024]{2,1,0:T(1,128)S(1)} all-gather(f32[1,1,1024]{2,1,0:T(1,128)S(1)} %get-tuple-element.102), channel_id=1, replica_groups=mesh['dp'=8,'rep'=4] {'dp'}, dimensions={0}, use_global_device_ids=true | all-gather | bytes 36864 | tf_op jit(solution)/shard_map/all_gather | solution.py:15
  155.1 8.9 %all-gather.11 = f32[8,1,1024]{2,1,0:T(1,128)S(1)} all-gather(f32[1,1,1024]{2,1,0:T(1,128)S(1)} %get-tuple-element.96), channel_id=1, replica_groups=mesh['dp'=8,'rep'=4] {'dp'}, dimensions={0}, use_global_device_ids=true | all-gather | bytes 36864 | tf_op jit(solution)/shard_map/all_gather | solution.py:15
  164.0 10.0 %all-gather.3 = bf16[1,1024,256]{2,1,0:T(8,128)(2,1)} all-gather(bf16[1,128,256]{2,1,0:T(8,128)(2,1)S(1)} %get-tuple-element.59), channel_id=5, replica_groups=mesh['dp'=8,'rep'=4] {'dp'}, dimensions={1}, use_global_device_ids=true | all-gather | bytes 589824 | tf_op jit(solution)/shard_map/all_gather | solution.py:44
  174.1 8.9 %all-gather.12 = f32[8,1,1024]{2,1,0:T(1,128)S(1)} all-gather(f32[1,1,1024]{2,1,0:T(1,128)S(1)} %get-tuple-element.101), channel_id=1, replica_groups=mesh['dp'=8,'rep'=4] {'dp'}, dimensions={0}, use_global_device_ids=true | all-gather | bytes 36864 | tf_op jit(solution)/shard_map/all_gather | solution.py:15
  183.0 8.5 %all-gather.13 = f32[8,1,1024]{2,1,0:T(1,128)S(1)} all-gather(f32[1,1,1024]{2,1,0:T(1,128)S(1)} %get-tuple-element.95), channel_id=1, replica_groups=mesh['dp'=8,'rep'=4] {'dp'}, dimensions={0}, use_global_device_ids=true | all-gather | bytes 36864 | tf_op jit(solution)/shard_map/all_gather | solution.py:15
  191.5 8.9 %all-gather.14 = f32[8,1,1024]{2,1,0:T(1,128)S(1)} all-gather(f32[1,1,1024]{2,1,0:T(1,128)S(1)} %get-tuple-element.100), channel_id=1, replica_groups=mesh['dp'=8,'rep'=4] {'dp'}, dimensions={0}, use_global_device_ids=true | all-gather | bytes 36864 | tf_op jit(solution)/shard_map/all_gather | solution.py:15
  200.5 8.3 %all-gather.15 = f32[8,1,1024]{2,1,0:T(1,128)S(1)} all-gather(f32[1,1,1024]{2,1,0:T(1,128)S(1)} %get-tuple-element.94), channel_id=1, replica_groups=mesh['dp'=8,'rep'=4] {'dp'}, dimensions={0}, use_global_device_ids=true | all-gather | bytes 36864 | tf_op jit(solution)/shard_map/all_gather | solution.py:15
  208.8 10.6 %all-gather.5 = bf16[1,256,1024]{2,1,0:T(8,128)(2,1)} all-gather(bf16[1,32,1024]{2,1,0:T(8,128)(2,1)S(1)} %get-tuple-element.57), channel_id=7, replica_groups=mesh['dp'=8,'rep'=4] {'dp'}, dimensions={1}, use_global_device_ids=true | all-gather | bytes 589824 | tf_op jit(solution)/shard_map/all_gather | solution.py:44
  219.5 8.3 %all-gather.16 = f32[8,1,1024]{2,1,0:T(1,128)S(1)} all-gather(f32[1,1,1024]{2,1,0:T(1,128)S(1)} %get-tuple-element.99), channel_id=1, replica_groups=mesh['dp'=8,'rep'=4] {'dp'}, dimensions={0}, use_global_device_ids=true | all-gather | bytes 36864 | tf_op jit(solution)/shard_map/all_gather | solution.py:15
  227.8 8.9 %all-gather.17 = f32[8,1,1024]{2,1,0:T(1,128)S(1)} all-gather(f32[1,1,1024]{2,1,0:T(1,128)S(1)} %get-tuple-element.93), channel_id=1, replica_groups=mesh['dp'=8,'rep'=4] {'dp'}, dimensions={0}, use_global_device_ids=true | all-gather | bytes 36864 | tf_op jit(solution)/shard_map/all_gather | solution.py:15
  236.7 2.1 constant_dynamic-update-slice_fusion.3
  242.0 5.4 %multiply_reduce_fusion.4 = (f32[256]{0:T(256)S(1)}, f32[256]{0:T(256)S(1)}, f32[1568,256]{1,0:T(8,128)S(1)}) fusion(bf16[1568,2304]{1,0:T(8,128)(2,1)} %constant_dynamic-update-slice_fusion, bf16[1,2304,256]{2,1,0:T(8,128)(2,1)} %all-gather.21.cloned.1.call-done), kind=kOutput, calls=%fused_computation.9 | convolution fusion | flops 1850891776 | bytes 10012672 | tf_op jit(solution)/shard_map/dot_general | solution.py:105
  247.4 8.4 %all-reduce.12 = (f32[256]{0:T(256)S(1)}, f32[256]{0:T(256)S(1)}) all-reduce(f32[256]{0:T(256)S(1)} %get-tuple-element.12, f32[256]{0:T(256)S(1)} %get-tuple-element.11), channel_id=1, replica_groups=mesh['dp'=8,'rep'=4] {'rep'}, use_global_device_ids=true, to_apply=%region_12.13 | all-reduce | flops 512 | bytes 4096 | tf_op jit(solution)/shard_map/psum | solution.py:50
  255.8 11.8 %all-reduce.6 = (f32[256]{0:T(256)S(1)}, f32[256]{0:T(256)S(1)}) all-reduce(f32[256]{0:T(256)S(1)} %get-tuple-element.35, f32[256]{0:T(256)S(1)} %get-tuple-element.36), channel_id=1, replica_groups=mesh['dp'=8,'rep'=4] {'dp'}, use_global_device_ids=true, to_apply=%region_13.14 | all-reduce | flops 512 | bytes 4096 | tf_op jit(solution)/shard_map/psum | solution.py:51
  268.2 3.8 multiply_reduce_fusion.1
  272.0 10.5 %all-reduce.11 = (f32[1024]{0:T(1024)S(1)}, f32[1024]{0:T(1024)S(1)}) all-reduce(f32[1024]{0:T(1024)S(1)} %get-tuple-element.6, f32[1024]{0:T(1024)S(1)} %get-tuple-element.5), channel_id=1, replica_groups=mesh['dp'=8,'rep'=4] {'rep'}, use_global_device_ids=true, to_apply=%region_20.21 | all-reduce | flops 2048 | bytes 16384 | tf_op jit(solution)/shard_map/psum | solution.py:50
  282.5 12.1 %all-reduce.5 = (f32[1024]{0:T(1024)S(1)}, f32[1024]{0:T(1024)S(1)}) all-reduce(f32[1024]{0:T(1024)S(1)} %get-tuple-element.33, f32[1024]{0:T(1024)S(1)} %get-tuple-element.34), channel_id=1, replica_groups=mesh['dp'=8,'rep'=4] {'dp'}, use_global_device_ids=true, to_apply=%region_21.22 | all-reduce | flops 2048 | bytes 16384 | tf_op jit(solution)/shard_map/psum | solution.py:51
  294.7 5.2 %maximum_convert_fusion.1 = bf16[1568,1024]{1,0:T(8,128)(2,1)S(1)} fusion(bf16[1568,1024]{1,0:T(8,128)(2,1)} %param.10, f32[1568,1024]{1,0:T(8,128)} %get-tuple-element.119, f32[1024]{0:T(1024)S(1)} %get-tuple-element.76, f32[1024]{0:T(1024)S(1)} %get-tuple-element.75), kind=kLoop, calls=%fused_computation.2 | loop fusion | flops 9633792 | bytes 12853248 | tf_op jit(solution)/shard_map/convert_element_type | solution.py:113
  299.9 2.2 multiply_reduce_fusion.3
  302.0 8.3 %all-reduce.10 = (f32[256]{0:T(256)S(1)}, f32[256]{0:T(256)S(1)}) all-reduce(f32[256]{0:T(256)S(1)} %get-tuple-element.10, f32[256]{0:T(256)S(1)} %get-tuple-element.9), channel_id=1, replica_groups=mesh['dp'=8,'rep'=4] {'rep'}, use_global_device_ids=true, to_apply=%region_28.29 | all-reduce | flops 512 | bytes 4096 | tf_op jit(solution)/shard_map/psum | solution.py:50
  310.4 12.0 %all-reduce.4 = (f32[256]{0:T(256)S(1)}, f32[256]{0:T(256)S(1)}) all-reduce(f32[256]{0:T(256)S(1)} %get-tuple-element.31, f32[256]{0:T(256)S(1)} %get-tuple-element.32), channel_id=1, replica_groups=mesh['dp'=8,'rep'=4] {'dp'}, use_global_device_ids=true, to_apply=%region_29.30 | all-reduce | flops 512 | bytes 4096 | tf_op jit(solution)/shard_map/psum | solution.py:51
  323.1 2.5 maximum_convert_fusion.3
  325.6 2.1 reshape.49
  327.7 7.0 %pad_slice_fusion = (bf16[8,14,14,256]{3,2,1,0:T(8,128)(2,1)}, bf16[8,14,14,256]{3,2,1,0:T(8,128)(2,1)}, bf16[8,14,14,256]{3,2,1,0:T(8,128)(2,1)}, bf16[8,14,14,...) fusion(bf16[8,14,14,256]{3,2,1,0:T(8,128)(2,1)} %reshape.49), kind=kLoop, calls=%fused_computation.24 | loop fusion | bytes 7225344 | tf_op jit(solution)/shard_map/slice | solution.py:24
  334.8 2.1 concatenate.73
  336.9 2.2 constant_dynamic-update-slice_fusion.17
  339.1 2.1 concatenate.74
  341.2 2.1 constant_dynamic-update-slice_fusion.16
  343.4 2.1 concatenate.75
  345.5 2.2 concatenate.76
  347.6 2.1 concatenate.77
  349.8 2.1 concatenate.78
  351.9 2.1 concatenate.79
  354.0 2.1 concatenate.80
  356.1 2.3 constant_dynamic-update-slice_fusion.15
  358.4 2.1 constant_dynamic-update-slice_fusion.14
  360.5 2.6 constant_dynamic-update-slice_fusion.13
  363.1 2.1 constant_dynamic-update-slice_fusion.12
  368.4 6.5 %multiply_reduce_fusion.2 = (f32[256]{0:T(256)S(1)}, f32[256]{0:T(256)S(1)}, f32[1568,256]{1,0:T(8,128)}) fusion(bf16[1568,2304]{1,0:T(8,128)(2,1)} %constant_dynamic-update-slice_fusion.9, bf16[1,2304,256]{2,1,0:T(8,128)(2,1)} %all-gather.23.cloned.1.call-done), kind=kOutput, calls=%fused_computation.5 | convolution fusion | flops 1850891776 | bytes 10012672 | tf_op jit(solution)/shard_map/dot_general | solution.py:105
  374.9 10.3 %all-reduce.9 = (f32[256]{0:T(256)S(1)}, f32[256]{0:T(256)S(1)}) all-reduce(f32[256]{0:T(256)S(1)} %get-tuple-element.8, f32[256]{0:T(256)S(1)} %get-tuple-element.7), channel_id=1, replica_groups=mesh['dp'=8,'rep'=4] {'rep'}, use_global_device_ids=true, to_apply=%region_36.37 | all-reduce | flops 512 | bytes 4096 | tf_op jit(solution)/shard_map/psum | solution.py:50
  385.3 11.8 %all-reduce.3 = (f32[256]{0:T(256)S(1)}, f32[256]{0:T(256)S(1)}) all-reduce(f32[256]{0:T(256)S(1)} %get-tuple-element.29, f32[256]{0:T(256)S(1)} %get-tuple-element.30), channel_id=1, replica_groups=mesh['dp'=8,'rep'=4] {'dp'}, use_global_device_ids=true, to_apply=%region_37.38 | all-reduce | flops 512 | bytes 4096 | tf_op jit(solution)/shard_map/psum | solution.py:51
  397.7 5.3 %multiply_reduce_fusion = (f32[1024]{0:T(1024)S(1)}, f32[1024]{0:T(1024)S(1)}, f32[1568,1024]{1,0:T(8,128)}) fusion(bf16[1,256,1024]{2,1,0:T(8,128)(2,1)} %all-gather.5, f32[1568,256]{1,0:T(8,128)} %get-tuple-element.121, f32[256]{0:T(256)S(1)} %get-tuple-element.78, f32[256]{0:T(256)S(1)} %get-tuple-element.77), kind=kOutput, calls=%fused_computation.1 | convolution fusion | flops 828504064 | bytes 8562688 | tf_op jit(solution)/shard_map/dot_general | solution.py:109
  403.0 8.5 %all-reduce.8 = (f32[1024]{0:T(1024)S(1)}, f32[1024]{0:T(1024)S(1)}) all-reduce(f32[1024]{0:T(1024)S(1)} %get-tuple-element.4, f32[1024]{0:T(1024)S(1)} %get-tuple-element.3), channel_id=1, replica_groups=mesh['dp'=8,'rep'=4] {'rep'}, use_global_device_ids=true, to_apply=%region_44.45 | all-reduce | flops 2048 | bytes 16384 | tf_op jit(solution)/shard_map/psum | solution.py:50
  411.5 12.1 %all-reduce.2 = (f32[1024]{0:T(1024)S(1)}, f32[1024]{0:T(1024)S(1)}) all-reduce(f32[1024]{0:T(1024)S(1)} %get-tuple-element.27, f32[1024]{0:T(1024)S(1)} %get-tuple-element.28), channel_id=1, replica_groups=mesh['dp'=8,'rep'=4] {'dp'}, use_global_device_ids=true, to_apply=%region_45.46 | all-reduce | flops 2048 | bytes 16384 | tf_op jit(solution)/shard_map/psum | solution.py:51
  423.7 5.8 %maximum_convert_fusion = bf16[1568,1024]{1,0:T(8,128)(2,1)} fusion(bf16[1568,1024]{1,0:T(8,128)(2,1)S(1)} %maximum_convert_fusion.1, f32[1568,1024]{1,0:T(8,128)} %get-tuple-element.122, f32[1024]{0:T(1024)S(1)} %get-tuple-element.74, f32[1024]{0:T(1024)S(1)} %get-tuple-element.73), kind=kLoop, calls=%fused_computation | loop fusion | flops 9633792 | bytes 12853248 | tf_op jit(solution)/shard_map/convert_element_type | solution.py:113
  (93 shorter events, 35.8 us)
Async XLA Ops:
  7.2 234.8 %all-gather.21.cloned.1.call-start = ((), (), s32[]{:S(2)}) async-start(), calls=%async_computation | async-start | bytes 1327104 | tf_op jit(solution)/shard_map/all_gather | solution.py:44
  9.0 359.4 %all-gather.23.cloned.1.call-start = ((), (), s32[]{:S(2)}) async-start(), calls=%async_computation.1 | async-start | bytes 1327104 | tf_op jit(solution)/shard_map/all_gather | solution.py:44
  86.8 0.6 copy-start.11
  86.8 0.6 copy-start.12
  118.7 120.2 %copy-start = (bf16[1568,256]{1,0:T(8,128)(2,1)S(1)}, bf16[1568,256]{1,0:T(8,128)(2,1)}, u32[]{:S(2)}) copy-start(bf16[1568,256]{1,0:T(8,128)(2,1)} %concatenate.69) | copy-start | bytes 2408452
  242.0 25.6 %copy-start.19 = (f32[1,256]{1,0:T(1,128)S(1)}, f32[1,256]{1,0:T(1,128)}, u32[]{:S(2)}) copy-start(f32[1,256]{1,0:T(1,128)} %get-tuple-element.67) | copy-start | bytes 3076
  242.0 25.6 %copy-start.20 = (f32[1,256]{1,0:T(1,128)S(1)}, f32[1,256]{1,0:T(1,128)}, u32[]{:S(2)}) copy-start(f32[1,256]{1,0:T(1,128)} %get-tuple-element.71) | copy-start | bytes 3076
  268.2 26.4 %copy-start.9 = (f32[1,1024]{1,0:T(1,128)S(1)}, f32[1,1024]{1,0:T(1,128)}, u32[]{:S(2)}) copy-start(f32[1,1024]{1,0:T(1,128)} %get-tuple-element.62) | copy-start | bytes 12292
  268.2 26.4 %copy-start.10 = (f32[1,1024]{1,0:T(1,128)S(1)}, f32[1,1024]{1,0:T(1,128)}, u32[]{:S(2)}) copy-start(f32[1,1024]{1,0:T(1,128)} %get-tuple-element.64) | copy-start | bytes 12292
  294.7 5.2 %copy-start.4 = (bf16[1,1024,256]{2,1,0:T(8,128)(2,1)S(1)}, bf16[1,1024,256]{2,1,0:T(8,128)(2,1)}, u32[]{:S(2)}) copy-start(bf16[1,1024,256]{2,1,0:T(8,128)(2,1)} %all-gather.3) | copy-start | bytes 1572868
  299.9 22.5 %copy-start.17 = (f32[1,256]{1,0:T(1,128)S(1)}, f32[1,256]{1,0:T(1,128)}, u32[]{:S(2)}) copy-start(f32[1,256]{1,0:T(1,128)} %get-tuple-element.66) | copy-start | bytes 3076
  299.9 22.5 %copy-start.18 = (f32[1,256]{1,0:T(1,128)S(1)}, f32[1,256]{1,0:T(1,128)}, u32[]{:S(2)}) copy-start(f32[1,256]{1,0:T(1,128)} %get-tuple-element.70) | copy-start | bytes 3076
  356.1 9.1 %copy-start.3 = (bf16[1568,256]{1,0:T(8,128)(2,1)S(1)}, bf16[1568,256]{1,0:T(8,128)(2,1)}, u32[]{:S(2)}) copy-start(bf16[1568,256]{1,0:T(8,128)(2,1)} %concatenate.78) | copy-start | bytes 2408452
  356.1 10.2 %copy-start.1 = (bf16[1568,256]{1,0:T(8,128)(2,1)S(1)}, bf16[1568,256]{1,0:T(8,128)(2,1)}, u32[]{:S(2)}) copy-start(bf16[1568,256]{1,0:T(8,128)(2,1)} %concatenate.79) | copy-start | bytes 2408452
  356.1 11.2 %copy-start.2 = (bf16[1568,256]{1,0:T(8,128)(2,1)S(1)}, bf16[1568,256]{1,0:T(8,128)(2,1)}, u32[]{:S(2)}) copy-start(bf16[1568,256]{1,0:T(8,128)(2,1)} %concatenate.80) | copy-start | bytes 2408452
  368.4 28.7 %copy-start.15 = (f32[1,256]{1,0:T(1,128)S(1)}, f32[1,256]{1,0:T(1,128)}, u32[]{:S(2)}) copy-start(f32[1,256]{1,0:T(1,128)} %get-tuple-element.65) | copy-start | bytes 3076
  368.4 28.7 %copy-start.16 = (f32[1,256]{1,0:T(1,128)S(1)}, f32[1,256]{1,0:T(1,128)}, u32[]{:S(2)}) copy-start(f32[1,256]{1,0:T(1,128)} %get-tuple-element.69) | copy-start | bytes 3076
  397.6 26.0 %copy-start.7 = (f32[1,1024]{1,0:T(1,128)S(1)}, f32[1,1024]{1,0:T(1,128)}, u32[]{:S(2)}) copy-start(f32[1,1024]{1,0:T(1,128)} %get-tuple-element.61) | copy-start | bytes 12292
  397.7 26.0 %copy-start.8 = (f32[1,1024]{1,0:T(1,128)S(1)}, f32[1,1024]{1,0:T(1,128)}, u32[]{:S(2)}) copy-start(f32[1,1024]{1,0:T(1,128)} %get-tuple-element.63) | copy-start | bytes 12292
  423.6 5.9 %copy-start.6 = (f32[1,1024]{1,0:T(1,128)S(1)}, f32[1,1024]{1,0:T(1,128)}, u32[]{:S(2)}) copy-start(f32[1,1024]{1,0:T(1,128)} %param.18) | copy-start | bytes 12292
  423.7 5.9 %copy-start.14 = (f32[256]{0:T(256)S(1)}, f32[256]{0:T(256)}, u32[]{:S(2)}) copy-start(f32[256]{0:T(256)} %get-tuple-element.85) | copy-start | bytes 3076
  423.7 7.7 %copy-start.5 = (f32[1,1024]{1,0:T(1,128)S(1)}, f32[1,1024]{1,0:T(1,128)}, u32[]{:S(2)}) copy-start(f32[1,1024]{1,0:T(1,128)} %param.17) | copy-start | bytes 12292
  423.7 7.7 %copy-start.13 = (f32[256]{0:T(256)S(1)}, f32[256]{0:T(256)}, u32[]{:S(2)}) copy-start(f32[256]{0:T(256)} %get-tuple-element.92) | copy-start | bytes 3076
Sparse Core Ops, SparseCore 0:
  9.9 26.7 all-gather.20
  38.5 23.9 all-gather.22
